TPU v7x, 32 devices: a whole 2x2x4 slice. The times are simulated.
32 devices in a mesh: row: 8 (over z, y), col: 4 (over x, core).
Axes of the slice: x: 2, y: 2, z: 4, core: 2. Of those that a mesh axis runs over, the one named last changes fastest.
Arguments:
- embeddings: float32 [32768, 2048], P('row', 'col'), may hold values from -2.5 to 2.5
- selected: int32 [512], replicated, may hold values from 0 to 32767, as said below
Outputs:
- sample_share: float32 [32768], P(('row', 'col'))
- log_gain: float32 [32768], P(('row', 'col'))
- logdet_mean: float32 [], replicated
Inputs may be any that keep to these rules, and one draw needn't show every extreme that they name: `selected`: 512 distinct item indices.
All inputs are finite; a program needn't handle non-finite values.
Results may differ from a plain program's by a relative error of at most 0.0003.
Values sent between devices are 32-bit elements; how exact they have to be, the bound alone decides.
No kernel may reach another device: no remote copies, remote signals or barrier semaphores. Data moves between devices by JAX's collectives and lax.ppermute only.
A program may use at most 64 MiB of HBM per device.

v0:
```python
import jax
import jax.numpy as jnp
from jax import lax
from jax.sharding import PartitionSpec as P

K = 512


def local(embeddings, selected):
    rows_here = embeddings.shape[0]
    my_index = lax.axis_index("row")
    first_row = my_index * rows_here
    offsets = selected - first_row
    inside = (offsets >= 0) & (offsets < rows_here)
    picked = jnp.take(embeddings, jnp.clip(offsets, 0, rows_here - 1), axis=0)
    picked = jnp.where(inside[:, None], picked, jnp.zeros_like(picked))
    chosen = lax.psum(picked, "row")
    partial_value = jnp.dot(chosen, chosen.T, precision=lax.Precision.HIGHEST)
    kernel = lax.psum(partial_value, "col")
    kernel = kernel + jnp.eye(K, dtype=jnp.float32)
    factor = jnp.linalg.cholesky(kernel)
    logdet_mean = 2.0 * jnp.sum(jnp.log(jnp.diagonal(factor))) / K
    whitened = jax.scipy.linalg.solve_triangular(factor, chosen, lower=True)
    whitened_full = lax.all_gather(whitened, "col", axis=1, tiled=True)
    regrouped = lax.all_to_all(embeddings, "col", split_axis=0, concat_axis=1, tiled=True)
    coordinates = jnp.dot(regrouped, whitened_full.T, precision=lax.Precision.HIGHEST)
    gain = jnp.sum(regrouped * regrouped, axis=1) + 1.0 - jnp.sum(coordinates * coordinates, axis=1)
    item_count = rows_here * lax.axis_size("row")
    grand_total = lax.psum(jnp.sum(gain), ("row", "col"))
    sample_share = gain * (item_count / grand_total)
    return (sample_share, jnp.log(gain), logdet_mean)


def solution(mesh):
    return jax.shard_map(
        local,
        mesh=mesh,
        in_specs=(P("row", "col"), P()),
        out_specs=(P(("row", "col")), P(("row", "col")), P()),
        check_vma=False,
    )
```

profile of v0, /device:TPU:0, one launch (start us, length us, event | category | flops | bytes accessed | tf_op | source)
XLA Modules:
  0.0 404.0 jit_solution(5842791233570516075)
XLA Ops:
  7.9 5.4 %gather_fusion = f32[512,512]{1,0:T(8,128)S(1)} fusion(f32[4096,512]{1,0:T(8,128)} %param.2, s32[1024]{0:T(1024)S(1)} %pad_clamp_fusion), kind=kCustom, calls=%fused_computation | custom fusion | bytes 2099200 | tf_op jit(solution)/shard_map/jit(_take)/gather | solution.py:15
  14.6 81.2 %all-reduce.4.cloned.1.call-done = f32[512,512]{1,0:T(8,128)} async-done(((f32[512,512]{1,0:T(8,128)}), f32[512,512]{1,0:T(8,128)}) %all-reduce.4.cloned.1.call-update) | async-done | bytes 1048592 | tf_op jit(solution)/shard_map/psum | solution.py:17
  95.8 4.6 %fusion.34 = f32[512,512]{0,1:T(8,128)} fusion(f32[512,512]{1,0:T(8,128)} %all-reduce.4.cloned.1.call-done), kind=kOutput, calls=%fused_computation.85 | convolution fusion | flops 1610612736 | bytes 2097152 | tf_op jit(solution)/shard_map/dot_general | solution.py:18
  100.4 5.7 %all-to-all-start = ((f32[4,1024,512]{2,1,0:T(8,128)}), f32[4,1024,512]{2,1,0:T(8,128)}, u32[]{:S(2)}, u32[]{:S(2)}) async-start(f32[4,1024,512]{2,1,0:T(8,128)} %bitcast.58), calls=%async_computation | async-start | bytes 16777216 | tf_op jit(solution)/shard_map/all_to_all | solution.py:25
  106.4 45.0 %all-reduce.6.cloned.1.call-done = f32[512,512]{0,1:T(8,128)} async-done(((f32[512,512]{0,1:T(8,128)}), f32[512,512]{0,1:T(8,128)}) %all-reduce.6.cloned.1.call-update) | async-done | bytes 1048592 | tf_op jit(solution)/shard_map/psum | solution.py:19
  155.6 11.7 %cholesky.102 = f32[128,128]{1,0:T(8,128)S(1)} custom-call(f32[128,128]{1,0:T(8,128)S(1)} %cholesky.260), custom_call_target="Cholesky" | custom-call | tf_op jit(solution)/shard_map/jit(cholesky)/cholesky | solution.py:21
  167.3 9.8 %custom-call.31 = f32[1,128,128]{1,2,0:T(8,128)S(1)} custom-call(f32[1,128,128]{2,1,0:T(8,128)S(1)} %get-tuple-element.34), custom_call_target="InvertDiagBlocksLowerTriangular" | custom-call | tf_op jit(solution)/shard_map/jit(cholesky)/cholesky | solution.py:21
  179.8 11.7 %cholesky.213 = f32[128,128]{1,0:T(8,128)S(1)} custom-call(f32[128,128]{1,0:T(8,128)S(1)} %cholesky.264), custom_call_target="Cholesky" | custom-call | tf_op jit(solution)/shard_map/jit(cholesky)/cholesky | solution.py:21
  191.6 10.3 %custom-call.32 = f32[1,128,128]{1,2,0:T(8,128)S(1)} custom-call(f32[1,128,128]{2,1,0:T(8,128)S(1)} %get-tuple-element.31), custom_call_target="InvertDiagBlocksLowerTriangular" | custom-call | tf_op jit(solution)/shard_map/jit(cholesky)/cholesky | solution.py:21
  203.4 11.7 %cholesky.234 = f32[128,128]{1,0:T(8,128)S(1)} custom-call(f32[128,128]{1,0:T(8,128)S(1)} %cholesky.269), custom_call_target="Cholesky" | custom-call | tf_op jit(solution)/shard_map/jit(cholesky)/cholesky | solution.py:21
  215.9 9.8 %custom-call.33 = f32[1,128,128]{1,2,0:T(8,128)S(1)} custom-call(f32[1,128,128]{2,1,0:T(8,128)S(1)} %get-tuple-element.28), custom_call_target="InvertDiagBlocksLowerTriangular" | custom-call | tf_op jit(solution)/shard_map/jit(cholesky)/cholesky | solution.py:21
  227.1 11.7 %cholesky.251 = f32[128,128]{1,0:T(8,128)S(1)} custom-call(f32[128,128]{1,0:T(8,128)S(1)} %convolution_subtract_fusion.5), custom_call_target="Cholesky" | custom-call | tf_op jit(solution)/shard_map/jit(cholesky)/cholesky | solution.py:21
  244.2 11.6 %while.1 = (s32[]{:T(128)}, f32[512,512]{1,0:T(8,128)}, s32[4,2]{0,1:T(2,128)S(1)}, f32[4,128,128]{2,1,0:T(8,128)S(1)}, s32[]{:T(128)}) while((s32[]{:T(128)}, f32[512,512]{1,0:T(8,128)}, s32[4,2]{0,1:T(2,128)S(1)}, f32[4,128,128]{2,1,0:T(8,128)S(1)}, s32[]{:T(128)}) %tuple.35), condition=%wide.while_cond, body=%wide.while_body.sunk | while | flops 2 | bytes 131189 | solution.py:23
  244.8 2.3 bitcast_dynamic-update-slice_fusion.2
  247.7 2.3 bitcast_dynamic-update-slice_fusion.2
  250.6 2.3 bitcast_dynamic-update-slice_fusion.2
  253.6 2.2 bitcast_dynamic-update-slice_fusion.2
  255.8 39.3 %custom-call.34 = f32[4,128,128]{1,2,0:T(8,128)S(1)} custom-call(f32[4,128,128]{2,1,0:T(8,128)S(1)} %get-tuple-element.10), custom_call_target="InvertDiagBlocksLowerTriangular" | custom-call | tf_op jit(solution)/shard_map/jit(_solve_triangular)/triangular_solve | solution.py:23
  302.0 4.5 %gather_fusion.1 = f32[512]{0:T(512)S(1)} fusion(f32[512,512]{1,0:T(8,128)S(1)} %get-tuple-element.20, s32[512]{0:T(512)S(1)} %bitcast.57), kind=kCustom, calls=%fused_computation.1 | custom fusion | bytes 8192 | tf_op jit(solution)/shard_map/jit(diagonal)/cond/branch_0_fun/gather | solution.py:22
  307.2 9.3 %copy.11 = f32[1024,4,512]{0,2,1:T(8,128)} copy(f32[1024,4,512]{2,0,1:T(8,128)} %bitcast.1) | data formatting | bytes 16777216 | tf_op jit(solution)/shard_map/all_to_all | solution.py:25
  316.4 4.0 multiply_reduce_fusion
  320.4 16.2 %all-gather.2.cloned.1.call-done = f32[512,2048]{1,0:T(8,128)} async-done(((f32[512,512]{1,0:T(8,128)}), f32[512,2048]{1,0:T(8,128)}) %all-gather.2.cloned.1.call-update) | async-done | bytes 4194320 | tf_op jit(solution)/shard_map/all_gather | solution.py:24
  336.6 17.3 %multiply_reduce_fusion.1 = f32[1024]{0:T(1024)S(1)} fusion(f32[512,2048]{1,0:T(8,128)} %all-gather.2.cloned.1.call-done, f32[1024,2048]{0,1:T(8,128)} %bitcast.59), kind=kOutput, calls=%fused_computation.5 | convolution fusion | flops 12885949440 | bytes 12587008 | tf_op jit(solution)/shard_map/dot_general | solution.py:26
  355.2 39.6 %psum.23 = f32[]{:T(128)} all-reduce(f32[]{:T(128)} %fusion.32), channel_id=1, replica_groups=mesh['row'=8,'col'=4] {'row','col'}, use_global_device_ids=true, to_apply=%region_13.14 | all-reduce | flops 1 | bytes 8 | tf_op jit(solution)/shard_map/psum | solution.py:29
  (58 shorter events, 26.7 us)
Async XLA Ops:
  7.2 88.6 %all-reduce.4.cloned.1.call-start = ((), (), s32[]{:S(2)}) async-start(), calls=%async_computation.1 | async-start | bytes 2097152 | tf_op jit(solution)/shard_map/psum | solution.py:17
  14.6 136.9 %all-reduce.6.cloned.1.call-start = ((), (), s32[]{:S(2)}) async-start(), calls=%async_computation.2 | async-start | bytes 2097152 | tf_op jit(solution)/shard_map/psum | solution.py:19
  100.4 206.8 %all-to-all-start = ((f32[4,1024,512]{2,1,0:T(8,128)}), f32[4,1024,512]{2,1,0:T(8,128)}, u32[]{:S(2)}, u32[]{:S(2)}) async-start(f32[4,1024,512]{2,1,0:T(8,128)} %bitcast.58), calls=%async_computation | async-start | bytes 16777216 | tf_op jit(solution)/shard_map/all_to_all | solution.py:25
  106.1 189.1 %copy-start = (f32[512,512]{1,0:T(8,128)S(1)}, f32[512,512]{1,0:T(8,128)}, u32[]{:S(2)}) copy-start(f32[512,512]{1,0:T(8,128)} %all-reduce.4.cloned.1.call-done) | copy-start | bytes 3145732
  106.1 230.6 %all-gather.2.cloned.1.call-start = ((), (), s32[]{:S(2)}) async-start(), calls=%async_computation.3 | async-start | bytes 5242880 | tf_op jit(solution)/shard_map/all_gather | solution.py:24
  154.6 1.0 copy-start.1
Sparse Core Ops, SparseCore 0:
  14.7 81.0 all-reduce.3
  100.5 50.9 all-reduce.5
  302.1 34.4 all-gather.1
where the time goes:
time: 408 us; the launch traced here: 404 us
  waiting for transfers between devices  142 us (35%)
  other arithmetic  131 us (32%)
  blocking collectives  39.6 us (10%)
  matrix products  33.1 us (8%)
  local copies, waits for them, and re-layouts  32.1 us (8%)
  between operations  19.3 us (5%)
  starting transfers between devices  6.08 us (1%)
    psum x1, waiting for transfers between devices, local(): chosen = lax.psum(picked, 'row')  81.2 us
    another operation x14, other arithmetic, local(): factor = jnp.linalg.cholesky(kernel)  79.1 us
    psum x1, waiting for transfers between devices, local(): kernel = lax.psum(partial_value, 'col')  45 us
    another operation x4, other arithmetic, local(): whitened = jax.scipy.linalg.solve_triangular(factor, chosen, lower=True)  41.6 us
    psum x1, blocking collectives, local(): grand_total = lax.psum(jnp.sum(gain), ('row', 'col'))  39.6 us
    dot_general x1, matrix products, local(): jnp.dot(regrouped, whitened_full.T, precision=lax.Precision.HIGHEST)  17.3 us
    all_gather x1, waiting for transfers between devices, local(): whitened_full = lax.all_gather(whitened, 'col', axis=1, tiled=True)  16.2 us
    another operation x12, local copies, waits for them, and re-layouts  11.5 us
  transfers between devices with their start and end apart: 4, of which 3 were waited for; matrix products, arithmetic and copies ran while one was open for 41% of the time, Pallas kernels for 0%

commit v1 on v0

--- a/solution.py
+++ b/solution.py
@@ -2,6 +2,7 @@
 import jax.numpy as jnp
 from jax import lax
 from jax.sharding import PartitionSpec as P
+from jax.lax import all_gather
 
 K = 512
 
@@ -16,7 +17,8 @@
     picked = jnp.where(inside[:, None], picked, jnp.zeros_like(picked))
     chosen = lax.psum(picked, "row")
     partial_value = jnp.dot(chosen, chosen.T, precision=lax.Precision.HIGHEST)
-    kernel = lax.psum(partial_value, "col")
+    link_the_chains = lambda load: jnp.sum(all_gather(load, axis_name="col"), 0)
+    kernel = link_the_chains(partial_value)
     kernel = kernel + jnp.eye(K, dtype=jnp.float32)
     factor = jnp.linalg.cholesky(kernel)
     logdet_mean = 2.0 * jnp.sum(jnp.log(jnp.diagonal(factor))) / K

time: 408 us -> 414 us (1.015)
  waiting for transfers between devices: 142 us -> 148 us
    all_gather x0 -> x1, waiting for transfers between devices: none -> 50.7 us  [local(): link_the_chains = lambda load: jnp.sum(all_gather(load, axis_name='col'), 0)]
    psum x1 -> x0, waiting for transfers between devices: 45 us -> none  [local(): kernel = lax.psum(partial_value, 'col')]
  transfers between devices with their start and end apart: 4 -> 4, of which waited for: 3 -> 3; matrix products, arithmetic and copies ran while one was open for 41% -> 40% of each run, Pallas kernels for 0% -> 0%
where the time goes in v1:
time: 414 us; the launch traced here: 410 us
  waiting for transfers between devices  148 us (36%)
  other arithmetic  132 us (32%)
  blocking collectives  39.6 us (10%)
  matrix products  33.1 us (8%)
  local copies, waits for them, and re-layouts  31.8 us (8%)
  between operations  19.2 us (5%)
  starting transfers between devices  6.08 us (1%)
    psum x1, waiting for transfers between devices, local(): chosen = lax.psum(picked, 'row')  81.2 us
    another operation x14, other arithmetic, local(): factor = jnp.linalg.cholesky(kernel)  79 us
    all_gather x1, waiting for transfers between devices, local(): link_the_chains = lambda load: jnp.sum(all_gather(load, axis_name='col'), 0)  50.7 us
    another operation x4, other arithmetic, local(): whitened = jax.scipy.linalg.solve_triangular(factor, chosen, lower=True)  41.7 us
    psum x1, blocking collectives, local(): grand_total = lax.psum(jnp.sum(gain), ('row', 'col'))  39.6 us
    dot_general x1, matrix products, local(): jnp.dot(regrouped, whitened_full.T, precision=lax.Precision.HIGHEST)  17.3 us
    all_gather x1, waiting for transfers between devices, local(): whitened_full = lax.all_gather(whitened, 'col', axis=1, tiled=True)  16.4 us
    another operation x12, local copies, waits for them, and re-layouts  11.5 us
  transfers between devices with their start and end apart: 4, of which 3 were waited for; matrix products, arithmetic and copies ran while one was open for 40% of the time, Pallas kernels for 0%

profile of v1, /device:TPU:0, one launch (start us, length us, event | category | flops | bytes accessed | tf_op | source)
XLA Modules:
  0.0 409.8 jit_solution(17591757986898578238)
XLA Ops:
  7.9 5.4 %gather_fusion = f32[512,512]{1,0:T(8,128)S(1)} fusion(f32[4096,512]{1,0:T(8,128)} %param.2, s32[1024]{0:T(1024)S(1)} %pad_clamp_fusion), kind=kCustom, calls=%fused_computation | custom fusion | bytes 2099200 | tf_op jit(solution)/shard_map/jit(_take)/gather | solution.py:16
  14.6 81.2 %all-reduce.3.cloned.1.call-done = f32[512,512]{1,0:T(8,128)} async-done(((f32[512,512]{1,0:T(8,128)}), f32[512,512]{1,0:T(8,128)}) %all-reduce.3.cloned.1.call-update) | async-done | bytes 1048592 | tf_op jit(solution)/shard_map/psum | solution.py:18
  95.8 4.5 %fusion.35 = f32[512,512]{1,0:T(8,128)} fusion(f32[512,512]{1,0:T(8,128)} %all-reduce.3.cloned.1.call-done), kind=kOutput, calls=%fused_computation.86 | convolution fusion | flops 1610612736 | bytes 2097152 | tf_op jit(solution)/shard_map/dot_general | solution.py:19
  100.3 5.7 %all-to-all-start = ((f32[4,1024,512]{2,1,0:T(8,128)}), f32[4,1024,512]{2,1,0:T(8,128)}, u32[]{:S(2)}, u32[]{:S(2)}) async-start(f32[4,1024,512]{2,1,0:T(8,128)} %bitcast.61), calls=%async_computation | async-start | bytes 16777216 | tf_op jit(solution)/shard_map/all_to_all | solution.py:27
  106.3 50.7 %all-gather.6.cloned.1.call-done = f32[2048,512]{1,0:T(8,128)} async-done(((f32[512,512]{1,0:T(8,128)}), f32[2048,512]{1,0:T(8,128)}) %all-gather.6.cloned.1.call-update) | async-done | bytes 4194320 | tf_op jit(solution)/shard_map/all_gather | solution.py:20
  157.1 2.8 reduce_sum.48
  161.5 11.7 %cholesky.102 = f32[128,128]{1,0:T(8,128)S(1)} custom-call(f32[128,128]{1,0:T(8,128)S(1)} %cholesky.260), custom_call_target="Cholesky" | custom-call | tf_op jit(solution)/shard_map/jit(cholesky)/cholesky | solution.py:23
  173.4 9.8 %custom-call.31 = f32[1,128,128]{1,2,0:T(8,128)S(1)} custom-call(f32[1,128,128]{2,1,0:T(8,128)S(1)} %get-tuple-element.34), custom_call_target="InvertDiagBlocksLowerTriangular" | custom-call | tf_op jit(solution)/shard_map/jit(cholesky)/cholesky | solution.py:23
  185.7 11.7 %cholesky.213 = f32[128,128]{1,0:T(8,128)S(1)} custom-call(f32[128,128]{1,0:T(8,128)S(1)} %cholesky.264), custom_call_target="Cholesky" | custom-call | tf_op jit(solution)/shard_map/jit(cholesky)/cholesky | solution.py:23
  197.5 10.3 %custom-call.32 = f32[1,128,128]{1,2,0:T(8,128)S(1)} custom-call(f32[1,128,128]{2,1,0:T(8,128)S(1)} %get-tuple-element.31), custom_call_target="InvertDiagBlocksLowerTriangular" | custom-call | tf_op jit(solution)/shard_map/jit(cholesky)/cholesky | solution.py:23
  209.4 11.7 %cholesky.234 = f32[128,128]{1,0:T(8,128)S(1)} custom-call(f32[128,128]{1,0:T(8,128)S(1)} %cholesky.269), custom_call_target="Cholesky" | custom-call | tf_op jit(solution)/shard_map/jit(cholesky)/cholesky | solution.py:23
  221.8 9.8 %custom-call.33 = f32[1,128,128]{1,2,0:T(8,128)S(1)} custom-call(f32[1,128,128]{2,1,0:T(8,128)S(1)} %get-tuple-element.28), custom_call_target="InvertDiagBlocksLowerTriangular" | custom-call | tf_op jit(solution)/shard_map/jit(cholesky)/cholesky | solution.py:23
  233.1 11.9 %cholesky.251 = f32[128,128]{1,0:T(8,128)S(1)} custom-call(f32[128,128]{1,0:T(8,128)S(1)} %convolution_subtract_fusion.5), custom_call_target="Cholesky" | custom-call | tf_op jit(solution)/shard_map/jit(cholesky)/cholesky | solution.py:23
  250.1 11.6 %while.1 = (s32[]{:T(128)}, f32[512,512]{1,0:T(8,128)}, s32[4,2]{0,1:T(2,128)S(1)}, f32[4,128,128]{2,1,0:T(8,128)S(1)}, s32[]{:T(128)}) while((s32[]{:T(128)}, f32[512,512]{1,0:T(8,128)}, s32[4,2]{0,1:T(2,128)S(1)}, f32[4,128,128]{2,1,0:T(8,128)S(1)}, s32[]{:T(128)}) %tuple.35), condition=%wide.while_cond, body=%wide.while_body.sunk | while | flops 2 | bytes 131189 | solution.py:25
  250.7 2.3 bitcast_dynamic-update-slice_fusion.2
  253.6 2.3 bitcast_dynamic-update-slice_fusion.2
  256.5 2.3 bitcast_dynamic-update-slice_fusion.2
  261.6 39.3 %custom-call.34 = f32[4,128,128]{1,2,0:T(8,128)S(1)} custom-call(f32[4,128,128]{2,1,0:T(8,128)S(1)} %get-tuple-element.10), custom_call_target="InvertDiagBlocksLowerTriangular" | custom-call | tf_op jit(solution)/shard_map/jit(_solve_triangular)/triangular_solve | solution.py:25
  307.9 8.8 %copy.10 = f32[1024,4,512]{0,2,1:T(8,128)} copy(f32[1024,4,512]{2,0,1:T(8,128)} %bitcast.1) | data formatting | bytes 16777216 | tf_op jit(solution)/shard_map/all_to_all | solution.py:27
  316.7 4.2 %multiply_reduce_fusion = f32[1024]{0:T(1024)S(1)} fusion(f32[4,1024,512]{2,1,0:T(8,128)} %all-to-all-done), kind=kLoop, calls=%fused_computation.4 | loop fusion | flops 4193280 | bytes 8392704 | tf_op jit(solution)/shard_map/reduce_sum | solution.py:29
  320.9 4.5 %gather_fusion.1 = f32[512]{0:T(512)S(1)} fusion(f32[512,512]{1,0:T(8,128)S(1)} %get-tuple-element.20, s32[512]{0:T(512)S(1)} %bitcast.60), kind=kCustom, calls=%fused_computation.1 | custom fusion | bytes 8192 | tf_op jit(solution)/shard_map/jit(diagonal)/cond/branch_0_fun/gather | solution.py:24
  326.0 16.4 %all-gather.4.cloned.1.call-done = f32[512,2048]{1,0:T(8,128)} async-done(((f32[512,512]{1,0:T(8,128)}), f32[512,2048]{1,0:T(8,128)}) %all-gather.4.cloned.1.call-update) | async-done | bytes 4194320 | tf_op jit(solution)/shard_map/all_gather | solution.py:26
  342.5 17.3 %multiply_reduce_fusion.1 = f32[1024]{0:T(1024)S(1)} fusion(f32[512,2048]{1,0:T(8,128)} %all-gather.4.cloned.1.call-done, f32[1024,2048]{0,1:T(8,128)} %bitcast.62), kind=kOutput, calls=%fused_computation.5 | convolution fusion | flops 12885949440 | bytes 12587008 | tf_op jit(solution)/shard_map/dot_general | solution.py:28
  361.1 39.6 %psum.15 = f32[]{:T(128)} all-reduce(f32[]{:T(128)} %fusion.33), channel_id=1, replica_groups=mesh['row'=8,'col'=4] {'row','col'}, use_global_device_ids=true, to_apply=%region_13.14 | all-reduce | flops 1 | bytes 8 | tf_op jit(solution)/shard_map/psum | solution.py:31
  (58 shorter events, 26.3 us)
Async XLA Ops:
  7.2 88.6 %all-reduce.3.cloned.1.call-start = ((), (), s32[]{:S(2)}) async-start(), calls=%async_computation.1 | async-start | bytes 2097152 | tf_op jit(solution)/shard_map/psum | solution.py:18
  14.6 142.5 %all-gather.6.cloned.1.call-start = ((), (), s32[]{:S(2)}) async-start(), calls=%async_computation.3 | async-start | bytes 5242880 | tf_op jit(solution)/shard_map/all_gather | solution.py:20
  100.3 207.6 %all-to-all-start = ((f32[4,1024,512]{2,1,0:T(8,128)}), f32[4,1024,512]{2,1,0:T(8,128)}, u32[]{:S(2)}, u32[]{:S(2)}) async-start(f32[4,1024,512]{2,1,0:T(8,128)} %bitcast.61), calls=%async_computation | async-start | bytes 16777216 | tf_op jit(solution)/shard_map/all_to_all | solution.py:27
  106.0 236.5 %all-gather.4.cloned.1.call-start = ((), (), s32[]{:S(2)}) async-start(), calls=%async_computation.2 | async-start | bytes 5242880 | tf_op jit(solution)/shard_map/all_gather | solution.py:26
  159.9 141.1 %copy-start = (f32[512,512]{1,0:T(8,128)S(1)}, f32[512,512]{1,0:T(8,128)}, u32[]{:S(2)}) copy-start(f32[512,512]{1,0:T(8,128)} %all-reduce.3.cloned.1.call-done) | copy-start | bytes 3145732
  160.4 1.1 copy-start.1
Sparse Core Ops, SparseCore 0:
  14.7 81.0 all-reduce.2
  100.4 56.6 all-gather.5
  308.0 34.4 all-gather.3
